TPU v7x, 32 devices: a whole 2x2x4 slice. The times are simulated.
32 devices in a mesh: grp: 2 (over y), bn: 16 (over z, x, core).
Axes of the slice: x: 2, y: 2, z: 4, core: 2. Of those that a mesh axis runs over, the one named last changes fastest.
Arguments:
- images: bfloat16 [32, 19, 19, 384], P(('grp', 'bn')), parts along dimension 0, may hold values from -56 to 56
- expand_weight: bfloat16 [384, 2304], P('bn'), may hold values from -0.3125 to 0.3125
- expand_gain: float32 [2304], replicated, may hold values from 0.5 to 2
- expand_shift: float32 [2304], replicated, may hold values from -3 to 3
- depth_weight: bfloat16 [25, 2304], replicated, may hold values from -1.25 to 1.25
- depth_gain: float32 [2304], replicated, may hold values from 0.5 to 2
- depth_shift: float32 [2304], replicated, may hold values from -3 to 3
- squeeze_weight: bfloat16 [2304, 96], replicated, may hold values from -0.125 to 0.125
- squeeze_bias: float32 [96], replicated, may hold values from -4 to 4
- excite_weight: bfloat16 [96, 2304], replicated, may hold values from -0.625 to 0.625
- excite_bias: float32 [2304], replicated, may hold values from -4 to 4
- project_weight: bfloat16 [2304, 384], P('bn'), may hold values from -0.125 to 0.125
- project_gain: float32 [384], replicated, may hold values from 0.5 to 2
- project_shift: float32 [384], replicated, may hold values from -3 to 3
- group_table: int32 [32], P('grp'), parts along dimension 0, may hold values from 0 to 1, as said below
Outputs:
- block_output: bfloat16 [32, 19, 19, 384], P(('grp', 'bn')), parts along dimension 0
There are 2 independent parts, one for each index of `grp`. A program takes and returns all parts, laid end to end along the dimension named above; an argument that names none is the same for every part. Nothing has to cross between parts.
Inputs may be any that keep to these rules, and one draw needn't show every extreme that they name: `group_table`: each of the 2 statistics groups holds at least 4 images, placed anywhere among the images.
All inputs are finite; a program needn't handle non-finite values.
Results may differ from a plain program's by a relative error of at most 0.0065.
Values may be sent and summed in bfloat16 or wider, within the bound.
A program may use at most 64 MiB of HBM per device.

v0:
```python
import jax
import jax.numpy as jnp
from jax import lax
from jax.sharding import PartitionSpec as P

KERNEL = 5
STAT_GROUPS = 2
epsilon = 0.001


def normalize(values, centre, inverse, gain, shift):
    return (values.astype(jnp.float32) - centre) * inverse * gain + shift


def depthwise(widened, depth_weight, height, breadth):
    spatial = widened.reshape(height, breadth, widened.shape[-1])
    margin = KERNEL // 2
    padded = jnp.pad(spatial, ((margin, margin), (margin, margin), (0, 0)))
    accumulated = jnp.zeros(spatial.shape, jnp.float32)
    for row_shift in range(KERNEL):
        for col_shift in range(KERNEL):
            window = padded[row_shift : row_shift + height, col_shift : col_shift + breadth]
            accumulated = accumulated + window.astype(jnp.float32) * depth_weight[
                row_shift * KERNEL + col_shift
            ].astype(jnp.float32)
    return accumulated.reshape(height * breadth, spatial.shape[-1]).astype(jnp.bfloat16)


def group_moments(values, selector, population):
    totals = jnp.sum(values, axis=0, dtype=jnp.float32)
    squares = jnp.sum(jnp.square(values.astype(jnp.float32)), axis=0)
    weighted = selector[:, None, None] * jnp.stack([totals, squares])[None]
    summed = lax.psum(weighted, "bn")
    picked = jnp.sum(selector[:, None, None] * summed, axis=0)
    centre = picked[0] / population
    spread = picked[1] / population - centre * centre
    return (centre, lax.rsqrt(spread + epsilon))


def on_device(
    images,
    expand_weight,
    expand_gain,
    expand_shift,
    depth_weight,
    depth_gain,
    depth_shift,
    squeeze_weight,
    squeeze_bias,
    excite_weight,
    excite_bias,
    project_weight,
    project_gain,
    project_shift,
    group_table,
):
    height, breadth, channels = (images.shape[1], images.shape[2], images.shape[3])
    pixels = height * breadth
    flattened = images.reshape(pixels, channels)
    device_rank = lax.axis_index("bn")
    ranks_all = jnp.arange(group_table.shape[0], dtype=jnp.int32)
    my_group = jnp.sum(jnp.where(ranks_all == device_rank, group_table, 0))
    members = jnp.sum((group_table == my_group).astype(jnp.float32))
    population = members * pixels
    selector = (jnp.arange(STAT_GROUPS, dtype=jnp.int32) == my_group).astype(jnp.float32)
    inputs = flattened
    expanded = jnp.dot(
        inputs,
        lax.all_gather(expand_weight, "bn", axis=0, tiled=True),
        preferred_element_type=jnp.float32,
    ).astype(jnp.bfloat16)
    centre, inverse = group_moments(expanded, selector, population)
    widened = jax.nn.silu(normalize(expanded, centre, inverse, expand_gain, expand_shift)).astype(
        jnp.bfloat16
    )
    filtered = depthwise(widened, depth_weight, height, breadth)
    centre, inverse = group_moments(filtered, selector, population)
    activated = jax.nn.silu(normalize(filtered, centre, inverse, depth_gain, depth_shift)).astype(
        jnp.bfloat16
    )
    pooled = (jnp.sum(activated, axis=0, dtype=jnp.float32) / pixels).astype(jnp.bfloat16)[None, :]
    squeezed = jax.nn.silu(
        jnp.dot(pooled, squeeze_weight, preferred_element_type=jnp.float32) + squeeze_bias
    ).astype(jnp.bfloat16)
    excitation = jax.nn.sigmoid(
        jnp.dot(squeezed, excite_weight, preferred_element_type=jnp.float32) + excite_bias
    )
    gated_input = (activated * excitation).astype(jnp.bfloat16)
    inputs = gated_input
    projected = jnp.dot(
        inputs,
        lax.all_gather(project_weight, "bn", axis=0, tiled=True),
        preferred_element_type=jnp.float32,
    ).astype(jnp.bfloat16)
    centre, inverse = group_moments(projected, selector, population)
    output = flattened.astype(jnp.float32) + normalize(
        projected, centre, inverse, project_gain, project_shift
    )
    return output.astype(jnp.bfloat16).reshape(images.shape)


def solution(mesh):
    return jax.shard_map(
        on_device,
        mesh=mesh,
        in_specs=(
            P(("grp", "bn"), None, None, None),
            P("bn", None),
            P(),
            P(),
            P(),
            P(),
            P(),
            P(),
            P(),
            P(),
            P(),
            P("bn", None),
            P(),
            P(),
            P("grp"),
        ),
        out_specs=P(("grp", "bn"), None, None, None),
        check_vma=False,
    )
```

profile of v0, /device:TPU:0, one launch (start us, length us, event | category | flops | bytes accessed | tf_op | source)
XLA Modules:
  0.0 257.8 jit_solution(15007953222312947867)
XLA Ops:
  6.5 0.7 all-gather.3.cloned.1.call-update
  7.3 0.7 all-gather.5.cloned.1.call-update
  8.0 1.3 fusion.15
  9.3 0.6 compare_convert_fusion.1
  10.0 1.9 fusion.16
  11.9 1.9 convert_reduce_fusion.27
  13.7 1.1 convert_reduce_fusion.26
  14.9 1.1 reshape.239
  16.6 36.0 %all-gather.3.cloned.1.call-done = bf16[384,2304]{1,0:T(8,128)(2,1)} async-done(((bf16[24,2304]{1,0:T(8,128)(2,1)}), bf16[384,2304]{1,0:T(8,128)(2,1)}) %all-gather.3.cloned.1.call-update) | async-done | bytes 1769488 | tf_op jit(solution)/shard_map/all_gather | solution.py:69
  52.5 3.7 %convert_reduce_fusion = (f32[2304]{0:T(1024)S(1)}, f32[2304]{0:T(1024)S(1)}, bf16[361,2304]{1,0:T(8,128)(2,1)}) fusion(bf16[361,384]{1,0:T(8,128)(2,1)S(1)} %reshape.239, bf16[384,2304]{1,0:T(8,128)(2,1)} %all-gather.3.cloned.1.call-done), kind=kOutput, calls=%fused_computation.2 | convolution fusion | flops 642933504 | bytes 3728640 | tf_op jit(solution)/shard_map/dot_general | solution.py:67
  56.4 59.8 %psum.21 = f32[2,2,2304]{2,1,0:T(2,128)S(1)} all-reduce(f32[2,2,2304]{2,1,0:T(2,128)S(1)} %broadcast_multiply_fusion.1), channel_id=1, replica_groups=mesh['grp'=2,'bn'=16] {'bn'}, use_global_device_ids=true, to_apply=%region_3.4 | all-reduce | flops 9216 | bytes 73728 | tf_op jit(solution)/shard_map/psum | solution.py:33
  116.2 0.1 multiply_reduce_fusion.3
  116.4 2.6 %fusion.9 = bf16[361,2304]{1,0:T(8,128)(2,1)S(1)} fusion(bf16[361,2304]{1,0:T(8,128)(2,1)} %get-tuple-element.43, f32[2304]{0:T(1024)S(1)} %copy-done.2, f32[2304]{0:T(1024)S(1)} %copy-done.3, f32[2304]{0:T(1024)S(1)} %get-tuple-element.39, f32[2304]{0:T(1024)S(1)} %get-tuple-element.38), kind=kLoop, calls=%fused_computation.17 | loop fusion | flops 8317440 | bytes 3363840 | tf_op jit(solution)/shard_map/convert_element_type | solution.py:73
  119.0 2.0 reshape.240
  121.0 32.3 %convert_reduce_fusion.2 = (f32[2304]{0:T(1024)S(1)}, f32[2304]{0:T(1024)S(1)}, bf16[19,19,2304]{2,1,0:T(8,128)(2,1)S(1)}) fusion(f32[2304]{0:T(1024)S(1)} %get-tuple-element.34, f32[2304]{0:T(1024)S(1)} %get-tuple-element.35, f32[2304]{0:T(1024)S(1)} %get-tuple-element.12, f32[2304]{0:T(1024)S(1)} %get-tuple-element.13, f32[2304]{0:T(1024)S(1)} %get-tuple-element.14, ...), kind=kLoop, calls=%fused_computation.20 | loop fusion | flops 65703168 | bytes 3575808 | tf_op jit(solution)/shard_map/reduce_sum | solution.py:30
  153.4 2.2 reshape.267
  155.7 57.9 %psum.22 = f32[2,2,2304]{2,1,0:T(2,128)S(1)} all-reduce(f32[2,2,2304]{2,1,0:T(2,128)S(1)} %broadcast_multiply_fusion), channel_id=1, replica_groups=mesh['grp'=2,'bn'=16] {'bn'}, use_global_device_ids=true, to_apply=%region_8.9 | all-reduce | flops 9216 | bytes 73728 | tf_op jit(solution)/shard_map/psum | solution.py:33
  213.6 0.1 multiply_reduce_fusion.2
  213.8 1.6 convert_reduce_fusion.1
  215.4 0.4 convolution_reduce_fusion
  215.9 3.9 %fusion.24 = (f32[384]{0:T(512)S(1)}, f32[384]{0:T(512)S(1)}, f32[361,384]{1,0:T(8,128)S(1)}) fusion(bf16[2304,384]{1,0:T(8,128)(2,1)} %all-gather.5.cloned.1.call-done, f32[2304]{0:T(1024)S(1)} %add_divide_fusion, f32[2304]{0:T(1024)S(1)} %copy-done.4, f32[2304]{0:T(1024)S(1)} %copy-done.5, f32[2304]{0:T(1024)S(1)} %get-tuple-element.37, ...), kind=kOutput, calls=%fused_computation.106 | convolution fusion | flops 649452672 | bytes 5700096 | tf_op jit(solution)/shard_map/dot_general | solution.py:90
  219.9 30.0 %psum.23 = f32[2,2,384]{2,1,0:T(2,128)S(1)} all-reduce(f32[2,2,384]{2,1,0:T(2,128)S(1)} %broadcast_multiply_fusion.2), channel_id=1, replica_groups=mesh['grp'=2,'bn'=16] {'bn'}, use_global_device_ids=true, to_apply=%region_13.14 | all-reduce | flops 1536 | bytes 12288 | tf_op jit(solution)/shard_map/psum | solution.py:33
  250.0 0.1 add_convert_fusion.1
  250.2 0.8 reshape.241
  (42 shorter events, 0.7 us)
Async XLA Ops:
  6.5 208.8 %copy-start = (bf16[96,2304]{1,0:T(8,128)(2,1)S(1)}, bf16[96,2304]{1,0:T(8,128)(2,1)}, u32[]{:S(2)}) copy-start(bf16[96,2304]{1,0:T(8,128)(2,1)} %param.24) | copy-start | bytes 1327108
  6.5 46.0 %all-gather.3.cloned.1.call-start = ((), (), s32[]{:S(2)}) async-start(), calls=%async_computation | async-start | bytes 1880064 | tf_op jit(solution)/shard_map/all_gather | solution.py:69
  7.3 208.6 %all-gather.5.cloned.1.call-start = ((), (), s32[]{:S(2)}) async-start(), calls=%async_computation.1 | async-start | bytes 1880064 | tf_op jit(solution)/shard_map/all_gather | solution.py:92
  16.5 99.8 %copy-start.2 = (f32[2304]{0:T(1024)S(1)}, f32[2304]{0:T(1024)}, u32[]{:S(2)}) copy-start(f32[2304]{0:T(1024)} %param.18) | copy-start | bytes 27652
  16.5 99.8 %copy-start.3 = (f32[2304]{0:T(1024)S(1)}, f32[2304]{0:T(1024)}, u32[]{:S(2)}) copy-start(f32[2304]{0:T(1024)} %param.17) | copy-start | bytes 27652
  153.3 60.4 %copy-start.4 = (f32[2304]{0:T(1024)S(1)}, f32[2304]{0:T(1024)}, u32[]{:S(2)}) copy-start(f32[2304]{0:T(1024)} %param.21) | copy-start | bytes 27652
  153.3 60.4 %copy-start.5 = (f32[2304]{0:T(1024)S(1)}, f32[2304]{0:T(1024)}, u32[]{:S(2)}) copy-start(f32[2304]{0:T(1024)} %param.20) | copy-start | bytes 27652
  153.3 62.0 %copy-start.1 = (bf16[2304,96]{0,1:T(8,128)(2,1)S(1)}, bf16[2304,96]{0,1:T(8,128)(2,1)}, u32[]{:S(2)}) copy-start(bf16[2304,96]{0,1:T(8,128)(2,1)} %param.22) | copy-start | bytes 1327108
  153.3 62.0 %copy-start.9 = (f32[96]{0:T(128)S(1)}, f32[96]{0:T(128)}, u32[]{:S(2)}) copy-start(f32[96]{0:T(128)} %param.23) | copy-start | bytes 1156
  153.4 62.5 %copy-start.6 = (f32[2304]{0:T(1024)S(1)}, f32[2304]{0:T(1024)}, u32[]{:S(2)}) copy-start(f32[2304]{0:T(1024)} %param.25) | copy-start | bytes 27652
  215.8 34.2 %copy-start.7 = (f32[384]{0:T(512)S(1)}, f32[384]{0:T(512)}, u32[]{:S(2)}) copy-start(f32[384]{0:T(512)} %param.28) | copy-start | bytes 4612
  215.8 34.2 %copy-start.8 = (f32[384]{0:T(512)S(1)}, f32[384]{0:T(512)}, u32[]{:S(2)}) copy-start(f32[384]{0:T(512)} %param.27) | copy-start | bytes 4612
Sparse Core Ops, SparseCore 0:
  9.5 42.9 all-gather.2
  54.7 39.2 all-gather.4
where the time goes:
time: 258 us
  blocking collectives  148 us (57%)
  other arithmetic  44.2 us (17%)
  waiting for transfers between devices  37.4 us (14%)
  between operations  14.3 us (6%)
  matrix products  8.06 us (3%)
  local copies, waits for them, and re-layouts  6.24 us (2%)
    psum x3, blocking collectives, group_moments(): summed = lax.psum(weighted, 'bn')  148 us
    all_gather x1, waiting for transfers between devices, on_device(): lax.all_gather(expand_weight, 'bn', axis=0, tiled=True)  36 us
    reduce_sum x1, other arithmetic, group_moments(): totals = jnp.sum(values, axis=0, dtype=jnp.float32)  32.3 us
  transfers between devices with their start and end apart: 2, of which 1 were waited for; matrix products, arithmetic and copies ran while one was open for 21% of the time, Pallas kernels for 0%

commit v1 on v0

--- a/solution.py
+++ b/solution.py
@@ -2,6 +2,7 @@
 import jax.numpy as jnp
 from jax import lax
 from jax.sharding import PartitionSpec as P
+from jax.lax import all_gather
 
 KERNEL = 5
 STAT_GROUPS = 2
@@ -30,7 +31,11 @@
     totals = jnp.sum(values, axis=0, dtype=jnp.float32)
     squares = jnp.sum(jnp.square(values.astype(jnp.float32)), axis=0)
     weighted = selector[:, None, None] * jnp.stack([totals, squares])[None]
-    summed = lax.psum(weighted, "bn")
+
+    def tails_fill(in_array):
+        return all_gather(in_array, "bn").sum(axis=0)
+
+    summed = tails_fill(weighted)
     picked = jnp.sum(selector[:, None, None] * summed, axis=0)
     centre = picked[0] / population
     spread = picked[1] / population - centre * centre

time: 258 us -> 172 us (0.67)
  blocking collectives: 148 us -> 59.6 us
    psum x3 -> x0, blocking collectives: 148 us -> none  [group_moments(): summed = lax.psum(weighted, 'bn')]
    all_gather x0 -> x3, blocking collectives: none -> 59.6 us  [tails_fill(): return all_gather(in_array, 'bn').sum(axis=0)]
  transfers between devices with their start and end apart: 2 -> 2, of which waited for: 1 -> 1; matrix products, arithmetic and copies ran while one was open for 21% -> 32% of each run, Pallas kernels for 0% -> 0%
where the time goes in v1:
time: 172 us; the launch traced here: 171 us
  blocking collectives  59.6 us (35%)
  other arithmetic  44.5 us (26%)
  waiting for transfers between devices  37.4 us (22%)
  between operations  14.3 us (8%)
  matrix products  9.07 us (5%)
  local copies, waits for them, and re-layouts  6.23 us (4%)
    all_gather x3, blocking collectives, tails_fill(): return all_gather(in_array, 'bn').sum(axis=0)  59.6 us
    all_gather x1, waiting for transfers between devices, on_device(): lax.all_gather(expand_weight, 'bn', axis=0, tiled=True)  36 us
    reduce_sum x1, other arithmetic, group_moments(): totals = jnp.sum(values, axis=0, dtype=jnp.float32)  32.2 us
    dot_general x1, matrix products, on_device(): jnp.dot(inputs, lax.all_gather(project_weight, 'bn', axis=0, tiled=True),...  3.9 us
    dot_general x1, matrix products, on_device(): jnp.dot(inputs, lax.all_gather(expand_weight, 'bn', axis=0, tiled=True),...  3.73 us
  transfers between devices with their start and end apart: 2, of which 1 were waited for; matrix products, arithmetic and copies ran while one was open for 32% of the time, Pallas kernels for 0%

profile of v1, /device:TPU:0, one launch (start us, length us, event | category | flops | bytes accessed | tf_op | source)
XLA Modules:
  0.0 171.2 jit_solution(2425344217353091036)
XLA Ops:
  6.5 0.7 all-gather.3.cloned.1.call-update
  7.3 0.7 all-gather.5.cloned.1.call-update
  8.0 1.3 fusion.15
  9.3 0.6 compare_convert_fusion.1
  10.0 1.9 %fusion.16 = f32[]{:T(128)} fusion(s32[16]{0:T(128)} %param.29, s32[]{:T(128)} %fusion.15), kind=kLoop, calls=%fused_computation.98 | loop fusion | flops 47 | bytes 72 | tf_op jit(solution)/shard_map/reduce_sum | solution.py:68
  11.9 1.9 %convert_reduce_fusion.27 = (f32[2304]{0:T(1024)S(1)}, f32[2304]{0:T(1024)S(1)}, f32[2304]{0:T(1024)S(1)}, f32[2304]{0:T(1024)S(1)}, f32[2304]{0:T(1024)S(1)}, /...) fusion(bf16[25,2304]{1,0:T(8,128)(2,1)} %param.19), kind=kLoop, calls=%fused_computation.84 | loop fusion | flops 43776 | bytes 262656 | tf_op jit(solution)/shard_map/convert_element_type | solution.py:26
  13.7 1.1 convert_reduce_fusion.26
  14.9 1.1 reshape.248
  16.6 36.0 %all-gather.3.cloned.1.call-done = bf16[384,2304]{1,0:T(8,128)(2,1)} async-done(((bf16[24,2304]{1,0:T(8,128)(2,1)}), bf16[384,2304]{1,0:T(8,128)(2,1)}) %all-gather.3.cloned.1.call-update) | async-done | bytes 1769488 | tf_op jit(solution)/shard_map/all_gather | solution.py:74
  52.5 3.7 %convert_reduce_fusion = (f32[2304]{0:T(1024)S(1)}, f32[2304]{0:T(1024)S(1)}, bf16[361,2304]{1,0:T(8,128)(2,1)}) fusion(bf16[361,384]{1,0:T(8,128)(2,1)S(1)} %reshape.248, bf16[384,2304]{1,0:T(8,128)(2,1)} %all-gather.3.cloned.1.call-done), kind=kOutput, calls=%fused_computation.2 | convolution fusion | flops 642933504 | bytes 3728640 | tf_op jit(solution)/shard_map/dot_general | solution.py:72
  56.4 21.4 %all_gather.19 = f32[16,2,2,2304]{3,2,1,0:T(2,128)S(1)} all-gather(f32[1,2,2,2304]{3,2,1,0:T(2,128)S(1)} %broadcast_multiply_fusion.1), channel_id=1, replica_groups=mesh['grp'=2,'bn'=16] {'bn'}, dimensions={0}, use_global_device_ids=true | all-gather | bytes 626688 | tf_op jit(solution)/shard_map/all_gather | solution.py:36
  77.8 0.2 reduce_sum.138
  78.1 2.6 %fusion.9 = bf16[361,2304]{1,0:T(8,128)(2,1)S(1)} fusion(bf16[361,2304]{1,0:T(8,128)(2,1)} %get-tuple-element.43, f32[2304]{0:T(1024)S(1)} %copy-done.1, f32[2304]{0:T(1024)S(1)} %copy-done.2, f32[2304]{0:T(1024)S(1)} %get-tuple-element.39, f32[2304]{0:T(1024)S(1)} %get-tuple-element.38), kind=kLoop, calls=%fused_computation.17 | loop fusion | flops 8317440 | bytes 3363840 | tf_op jit(solution)/shard_map/convert_element_type | solution.py:78
  80.8 2.0 %reshape.249 = bf16[19,19,2304]{2,1,0:T(8,128)(2,1)} reshape(bf16[361,2304]{1,0:T(8,128)(2,1)S(1)} %fusion.9) | data formatting | bytes 3326976 | tf_op jit(solution)/shard_map/reshape | solution.py:17
  82.8 32.2 %convert_reduce_fusion.2 = (f32[2304]{0:T(1024)S(1)}, f32[2304]{0:T(1024)S(1)}, bf16[19,19,2304]{2,1,0:T(8,128)(2,1)S(1)}) fusion(f32[2304]{0:T(1024)S(1)} %get-tuple-element.34, f32[2304]{0:T(1024)S(1)} %get-tuple-element.35, f32[2304]{0:T(1024)S(1)} %get-tuple-element.12, f32[2304]{0:T(1024)S(1)} %get-tuple-element.13, f32[2304]{0:T(1024)S(1)} %get-tuple-element.14, ...), kind=kLoop, calls=%fused_computation.20 | loop fusion | flops 65703168 | bytes 3575808 | tf_op jit(solution)/shard_map/reduce_sum | solution.py:31
  115.0 2.2 %reshape.276 = f32[361,2304]{1,0:T(8,128)} reshape(bf16[19,19,2304]{2,1,0:T(8,128)(2,1)S(1)} %get-tuple-element.42) | data formatting | bytes 4990464 | tf_op jit(solution)/shard_map/convert_element_type | solution.py:13
  117.4 19.2 %all_gather.20 = f32[16,2,2,2304]{3,2,1,0:T(2,128)S(1)} all-gather(f32[1,2,2,2304]{3,2,1,0:T(2,128)S(1)} %broadcast_multiply_fusion), channel_id=1, replica_groups=mesh['grp'=2,'bn'=16] {'bn'}, dimensions={0}, use_global_device_ids=true | all-gather | bytes 626688 | tf_op jit(solution)/shard_map/all_gather | solution.py:36
  136.6 0.2 reduce_sum.143
  137.0 1.6 convert_reduce_fusion.1
  138.6 1.4 convolution_reduce_fusion
  140.1 3.9 %fusion.24 = (f32[384]{0:T(512)S(1)}, f32[384]{0:T(512)S(1)}, f32[361,384]{1,0:T(8,128)S(1)}) fusion(bf16[2304,384]{1,0:T(8,128)(2,1)} %all-gather.5.cloned.1.call-done, f32[2304]{0:T(1024)S(1)} %add_divide_fusion, f32[2304]{0:T(1024)S(1)} %copy-done.3, f32[2304]{0:T(1024)S(1)} %copy-done.4, f32[2304]{0:T(1024)S(1)} %get-tuple-element.37, ...), kind=kOutput, calls=%fused_computation.106 | convolution fusion | flops 649452672 | bytes 5700096 | tf_op jit(solution)/shard_map/dot_general | solution.py:95
  144.1 19.0 %all_gather.22 = f32[16,2,2,384]{3,2,1,0:T(2,128)S(1)} all-gather(f32[1,2,2,384]{3,2,1,0:T(2,128)S(1)} %broadcast_multiply_fusion.2), channel_id=1, replica_groups=mesh['grp'=2,'bn'=16] {'bn'}, dimensions={0}, use_global_device_ids=true | all-gather | bytes 104448 | tf_op jit(solution)/shard_map/all_gather | solution.py:36
  163.3 0.1 add_convert_fusion.1
  163.5 0.8 reshape.250
  (43 shorter events, 0.9 us)
Async XLA Ops:
  6.5 132.0 %copy-start = (bf16[96,2304]{1,0:T(8,128)(2,1)S(1)}, bf16[96,2304]{1,0:T(8,128)(2,1)}, u32[]{:S(2)}) copy-start(bf16[96,2304]{1,0:T(8,128)(2,1)} %param.24) | copy-start | bytes 1327108
  6.5 46.0 %all-gather.3.cloned.1.call-start = ((), (), s32[]{:S(2)}) async-start(), calls=%async_computation | async-start | bytes 1880064 | tf_op jit(solution)/shard_map/all_gather | solution.py:74
  7.3 132.9 %all-gather.5.cloned.1.call-start = ((), (), s32[]{:S(2)}) async-start(), calls=%async_computation.1 | async-start | bytes 1880064 | tf_op jit(solution)/shard_map/all_gather | solution.py:97
  16.5 61.6 %copy-start.1 = (f32[2304]{0:T(1024)S(1)}, f32[2304]{0:T(1024)}, u32[]{:S(2)}) copy-start(f32[2304]{0:T(1024)} %param.18) | copy-start | bytes 27652
  16.5 61.6 %copy-start.2 = (f32[2304]{0:T(1024)S(1)}, f32[2304]{0:T(1024)}, u32[]{:S(2)}) copy-start(f32[2304]{0:T(1024)} %param.17) | copy-start | bytes 27652
  115.0 22.0 %copy-start.3 = (f32[2304]{0:T(1024)S(1)}, f32[2304]{0:T(1024)}, u32[]{:S(2)}) copy-start(f32[2304]{0:T(1024)} %param.21) | copy-start | bytes 27652
  115.0 22.0 %copy-start.4 = (f32[2304]{0:T(1024)S(1)}, f32[2304]{0:T(1024)}, u32[]{:S(2)}) copy-start(f32[2304]{0:T(1024)} %param.20) | copy-start | bytes 27652
  115.0 23.6 %copy-start.8 = (f32[96]{0:T(128)S(1)}, f32[96]{0:T(128)}, u32[]{:S(2)}) copy-start(f32[96]{0:T(128)} %param.23) | copy-start | bytes 1156
  117.2 22.8 %copy-start.5 = (f32[2304]{0:T(1024)S(1)}, f32[2304]{0:T(1024)}, u32[]{:S(2)}) copy-start(f32[2304]{0:T(1024)} %param.25) | copy-start | bytes 27652
  140.1 23.3 %copy-start.6 = (f32[384]{0:T(512)S(1)}, f32[384]{0:T(512)}, u32[]{:S(2)}) copy-start(f32[384]{0:T(512)} %param.28) | copy-start | bytes 4612
  140.1 23.3 %copy-start.7 = (f32[384]{0:T(512)S(1)}, f32[384]{0:T(512)}, u32[]{:S(2)}) copy-start(f32[384]{0:T(512)} %param.27) | copy-start | bytes 4612
Sparse Core Ops, SparseCore 0:
  9.5 42.9 all-gather.2
  54.7 39.7 all-gather.4
